TPU v7x, 8 devices: a whole 2x2x1 slice. The times are simulated.
8 devices in a mesh: rep: 2 (over y, z), dp: 4 (over x, core).
Axes of the slice: x: 2, y: 2, z: 1, core: 2. Of those that a mesh axis runs over, the one named last changes fastest.
Arguments:
- a: bfloat16 [8, 4, 4096, 1280], P(('rep', 'dp')), parts along dimension 0
- g: bfloat16 [8, 4, 4096, 4096], P(('rep', 'dp')), parts along dimension 0
Outputs:
- output: bfloat16 [8, 1280, 4096], P('rep'), parts along dimension 0
There are 2 independent parts. A program takes and returns all parts, laid end to end along the dimension named above; each array names one.
All inputs are finite; a program needn't handle non-finite values.
Results may differ from a plain program's by a relative error of at most 0.012.
Values are sent between devices in bfloat16 or wider.
A program may use at most 2 GiB of HBM per device.

v0:
```python
import jax
import jax.numpy as jnp


def solution(mesh):
    groups = mesh.shape["rep"]

    def step(a, g):
        a, g = (t.reshape(groups, -1, *t.shape[1:]) for t in (a, g))
        sums = jnp.einsum("rsntd,rsntf->rndf", a, g, preferred_element_type=jnp.float32)
        return sums.astype(jnp.bfloat16).reshape(-1, *sums.shape[2:])

    return step
```

profile of v0, /device:TPU:0, one launch (start us, length us, event | category | flops | bytes accessed | tf_op | source)
XLA Modules:
  0.0 1597.2 jit_solution(5205749537207016753)
XLA Ops:
  0.0 187.7 %fusion.2 = f32[1,4,1280,4096]{3,2,1,0:T(8,128)} fusion(bf16[1,4,4096,4096]{3,2,1,0:T(8,128)(2,1)} %param.1, bf16[1,4,4096,1280]{3,2,1,0:T(8,128)(2,1)} %param), kind=kOutput, calls=%fused_computation.2 | convolution fusion | flops 171798691840 | bytes 260046848 | tf_op jit(solution)/rsntd,rsntf->rndf/dot_general | solution.py:10
  187.7 1409.5 %all-reduce.2 = bf16[1,4,1280,4096]{3,2,1,0:T(8,128)(2,1)} all-reduce(f32[1,4,1280,4096]{3,2,1,0:T(8,128)} %fusion.2), channel_id=1, replica_groups=[2,4]<=[8], use_global_device_ids=true, to_apply=%add.clone | all-reduce | flops 20971520 | bytes 125829120 | tf_op jit(solution)/rsntd,rsntf->rndf/dot_general | solution.py:10
where the time goes:
time: 1600 us
  blocking collectives  1410 us (88%)
  matrix products  188 us (12%)
    dot_general x1, blocking collectives, step(): jnp.einsum('rsntd,rsntf->rndf', a, g, preferred_element_type=jnp.float32)  1410 us
    dot_general x1, matrix products, step(): jnp.einsum('rsntd,rsntf->rndf', a, g, preferred_element_type=jnp.float32)  188 us

commit v1 on v0

v1 whole, which is shorter than its diff:
```python
import jax
import jax.numpy as jnp
from jax import lax
from jax.experimental import pallas as pl
from jax.experimental.pallas import tpu as pltpu
from jax.sharding import PartitionSpec as P

MESH = pl.DeviceIdType.MESH
N, TOK, D, FF = 4, 4096, 1280, 4096
RB, CB = 256, 512
HB = RB // 2
NR, NC = D // RB, FF // CB
PIECES = N * NC * NR
KT = 512
LAG = 24
QX = LAG + 2
QD = 4
QP = 3
QF = 4


def when(cond):
    return pl.when(cond)


def kernel(a, g, res, at, abuf, gbuf, prod, dsend, drecv, xsend, xrecv, fin,
           a_sem, g_sem, ds_sem, dr_sem, xs_sem, xr_sem, fl_sem, fs_sem, fr_sem,
           dfree, xfree):
    rep, me = lax.axis_index("rep"), lax.axis_index("dp")
    core = lax.rem(me, 2)
    sibling = (rep, me + 1 - 2 * core)
    partner = (rep, lax.rem(me + 2, 4))
    mine = pl.multiple_of(core * HB, HB)
    other = pl.multiple_of((1 - core) * HB, HB)

    def load_a(t):
        n, r = t // NR, lax.rem(t, NR)
        s = lax.rem(t, 2)
        cols = pl.ds(pl.multiple_of(r * RB, RB), RB)
        return pltpu.make_async_copy(a.at[n, :, cols], abuf.at[s], a_sem.at[s])

    def load_g(q):
        n, c = q // NC, lax.rem(q, NC)
        s = lax.rem(q, 2)
        cols = pl.ds(pl.multiple_of(c * CB, CB), CB)
        return pltpu.make_async_copy(g.at[n, :, cols], gbuf.at[s], g_sem.at[s])

    def across_cores(k):
        s = lax.rem(k, QD)
        return pltpu.make_async_remote_copy(
            dsend.at[s], drecv.at[s], ds_sem.at[s], dr_sem.at[s],
            device_id=sibling, device_id_type=MESH)

    def across_chips(k):
        s = lax.rem(k, QX)
        return pltpu.make_async_remote_copy(
            xsend.at[s], xrecv.at[s], xs_sem.at[s], xr_sem.at[s],
            device_id=partner, device_id_type=MESH)

    def place(k):
        q = k // NR
        n, c, r = q // NC, lax.rem(q, NC), lax.rem(k, NR)
        rows = pl.ds(pl.multiple_of(r * RB + mine, HB), HB)
        cols = pl.ds(pl.multiple_of(c * CB, CB), CB)
        return res.at[n, rows, cols]

    def keep(k):
        s = lax.rem(k, QF)
        return pltpu.make_async_copy(fin.at[s], place(k), fl_sem.at[s])

    def share(k):
        s = lax.rem(k, QF)
        return pltpu.make_async_remote_copy(
            fin.at[s], place(k), fs_sem.at[s], fr_sem,
            device_id=sibling, device_id_type=MESH)

    def multiply(k):
        q, r = k // NR, lax.rem(k, NR)
        n, c = q // NC, lax.rem(q, NC)
        gs = lax.rem(q, 2)

        @when(c == 0)
        def _():
            t = n * NR + r
            s = lax.rem(t, 2)
            load_a(t).wait()

            @pl.loop(0, TOK // KT)
            def _(i):
                toks = pl.ds(pl.multiple_of(i * KT, KT), KT)
                at[r, :, toks] = abuf[s, toks, :].T

            @when(t + 2 < N * NR)
            def _():
                load_a(t + 2).start()

        @when(r == 0)
        def _():
            load_g(q).wait()

        p = lax.rem(k, QP)
        prod[p] = jnp.dot(at[r], gbuf[gs], preferred_element_type=jnp.float32)

        @when((r == NR - 1) & (q + 2 < N * NC))
        def _():
            load_g(q + 2).start()

        @when(k >= QD)
        def _():
            across_cores(k - QD).wait_send()
            pl.semaphore_wait(dfree, 1)

        dsend[lax.rem(k, QD)] = prod[p, pl.ds(other, HB)].astype(jnp.bfloat16)
        across_cores(k).start()

    def chip_sum(k):
        across_cores(k).wait_recv()
        total = prod[lax.rem(k, QP), pl.ds(mine, HB)] + drecv[lax.rem(k, QD)].astype(jnp.float32)
        xsend[lax.rem(k, QX)] = total.astype(jnp.bfloat16)

        @when(k + QD < PIECES)
        def _():
            pl.semaphore_signal(dfree, inc=1, device_id=sibling, device_id_type=MESH)

        @when(k >= QX)
        def _():
            pl.semaphore_wait(xfree, 1)

        across_chips(k).start()

    def finish(k):
        across_chips(k).wait()

        @when(k >= QF)
        def _():
            keep(k - QF).wait()
            share(k - QF).wait_send()

        s = lax.rem(k, QX)
        total = xsend[s].astype(jnp.float32) + xrecv[s].astype(jnp.float32)
        fin[lax.rem(k, QF)] = total.astype(jnp.bfloat16)

        @when(k + QX < PIECES)
        def _():
            pl.semaphore_signal(xfree, inc=1, device_id=partner, device_id_type=MESH)

        keep(k).start()
        share(k).start()

    load_a(0).start()
    load_g(0).start()
    load_a(1).start()
    load_g(1).start()
    barrier = pltpu.get_barrier_semaphore()
    for peer in (sibling, partner):
        pl.semaphore_signal(barrier, inc=1, device_id=peer, device_id_type=MESH)
    pl.semaphore_wait(barrier, 2)

    @pl.loop(0, PIECES + LAG)
    def _(k):
        @when(k < PIECES)
        def _():
            multiply(k)

        @when((k != 1) & (k <= PIECES))
        def _():
            chip_sum(jnp.maximum(k - 1, 0))

        @when(k >= LAG)
        def _():
            finish(k - LAG)

    @pl.loop(PIECES - QD, PIECES)
    def _(k):
        across_cores(k).wait_send()

    @pl.loop(PIECES - QF, PIECES)
    def _(k):
        keep(k).wait()
        share(k).wait_send()

    half = res.at[pl.ds(0, N // 2)]
    pltpu.make_async_copy(half, half, fr_sem).wait()


def solution(mesh):
    dma, vmem, bf16 = pltpu.SemaphoreType.DMA, pltpu.VMEM, jnp.bfloat16
    anyspace = pl.BlockSpec(memory_space=pl.ANY)
    call = pl.pallas_call(
        kernel,
        out_shape=jax.ShapeDtypeStruct((N, D, FF), bf16),
        in_specs=[anyspace, anyspace],
        out_specs=anyspace,
        scratch_shapes=[
            vmem((NR, RB, TOK), bf16),
            vmem((2, TOK, RB), bf16),
            vmem((2, TOK, CB), bf16),
            vmem((QP, RB, CB), jnp.float32),
            vmem((QD, HB, CB), bf16),
            vmem((QD, HB, CB), bf16),
            vmem((QX, HB, CB), bf16),
            vmem((QX, HB, CB), bf16),
            vmem((QF, HB, CB), bf16),
            dma((2,)), dma((2,)), dma((QD,)), dma((QD,)), dma((QX,)), dma((QX,)),
            dma((QF,)), dma((QF,)), dma(()),
            pltpu.SemaphoreType.REGULAR, pltpu.SemaphoreType.REGULAR,
        ],
        compiler_params=pltpu.CompilerParams(
            collective_id=0, has_side_effects=True, vmem_limit_bytes=60 * 2**20),
        cost_estimate=pl.CostEstimate(
            flops=2 * N * TOK * D * FF, bytes_accessed=2 * N * (TOK * (D + FF) + D * FF),
            transcendentals=0),
    )

    def step(a, g):
        return call(a[0], g[0])

    return jax.shard_map(
        step, mesh=mesh, in_specs=(P(("rep", "dp")), P(("rep", "dp"))),
        out_specs=P("rep"), check_vma=False)
```

time: 1600 us -> 491 us (0.31)
  blocking collectives: 1410 us -> 0 us
  Pallas kernels: 0 us -> 463 us
  matrix products: 188 us -> 0 us
  local copies, waits for them, and re-layouts: 0 us -> 28.2 us
    dot_general x1 -> x0, blocking collectives: 1410 us -> none  [step(): jnp.einsum('rsntd,rsntf->rndf', a, g, preferred_element_type=jnp.float32)]
    pallas_call x0 -> x1, Pallas kernels: none -> 463 us  [step(): return call(a[0], g[0])]
    dot_general x1 -> x0, matrix products: 188 us -> none  [step(): jnp.einsum('rsntd,rsntf->rndf', a, g, preferred_element_type=jnp.float32)]
    unnamed x0 -> x1, local copies, waits for them, and re-layouts: none -> 28.2 us
where the time goes in v1:
time: 491 us
  Pallas kernels  463 us (94%)
  local copies, waits for them, and re-layouts  28.2 us (6%)
    pallas_call x1, Pallas kernels, step(): return call(a[0], g[0])  463 us
    unnamed x1, local copies, waits for them, and re-layouts  28.2 us

profile of v1, /device:TPU:0, one launch (start us, length us, event | category | flops | bytes accessed | tf_op | source)
XLA Modules:
  0.0 490.8 jit_solution(151301000592963093)
XLA Ops:
  0.0 462.6 %shard_map.28 = bf16[4,1280,4096]{2,1,0:T(8,128)(2,1)} custom-call(bf16[4,4096,1280]{2,1,0:T(8,128)(2,1)} %bitcast.2, bf16[4,4096,4096]{2,1,0:T(8,128)(2,1)} %bitcast.1.g), custom_call_target="tpu_custom_call" | custom-call | flops 171798691840 | bytes 218103808 | tf_op jit(solution)/shard_map/pallas_call | solution.py:216
  462.6 28.2 %copy.4 = bf16[4,1280,4096]{2,1,0:T(8,128)(2,1)} copy(bf16[4,1280,4096]{2,1,0:T(8,128)(2,1)} %shard_map.28) | data formatting | bytes 83886080

commit v2 on v1

v2 whole, which is shorter than its diff:
```python
import functools

import jax
import jax.numpy as jnp
from jax import lax
from jax.experimental import pallas as pl
from jax.experimental.pallas import tpu as pltpu
from jax.sharding import PartitionSpec as P


MESH = pl.DeviceIdType.MESH
N, TOK, D, FF = 4, 4096, 1280, 4096
RB, CB = 256, 512
HC = CB // 2
HB = RB // 2
NR, NC = D // RB, FF // CB
PIECES = N * NC * NR
TAILS = (13, 2)
LATE = PIECES - sum(TAILS) - 1
INSIDE = LATE
KT = 512
LAG = 24
QX = LAG + 2
QD = 4
QP = 3
QF = 4


GROUPS = tuple((PIECES - sum(TAILS[i:]), PIECES - sum(TAILS[i + 1:])) for i in range(len(TAILS)))
MOVES, REST = INSIDE // NR, INSIDE % NR
QM = 8


def when(cond):
    return pl.when(cond)


def where(k):
    q = k // NR
    return q // NC, lax.rem(k, NR), lax.rem(q, NC)


def kernel(a, g, res, own0, own1, own2, sib0, sib1, sib2, got0, at, abuf, gbuf, prod, dsend, drecv, xsend, xrecv, fin, lsend, lrecv, lsum,
           a_sem, g_sem, ds_sem, dr_sem, xs_sem, xr_sem, fl_sem, fs_sem, fr_sem,
           to_sem, ts_sem, tr_sem, late_sem, dfree, xfree):
    rep, me = lax.axis_index("rep"), lax.axis_index("dp")
    core = lax.rem(me, 2)
    sibling = (rep, me + 1 - 2 * core)
    partner = (rep, lax.rem(me + 2, 4))
    mine = pl.multiple_of(core * HB, HB)
    other = pl.multiple_of((1 - core) * HB, HB)

    def load_a(t):
        n, r = t // NR, lax.rem(t, NR)
        s = lax.rem(t, 2)
        cols = pl.ds(pl.multiple_of(r * RB, RB), RB)
        return pltpu.make_async_copy(a.at[n, :, cols], abuf.at[s], a_sem.at[s])

    def load_g(q, h):
        n, c = q // NC, lax.rem(q, NC)
        s = lax.rem(q, 2)
        cols = pl.ds(pl.multiple_of(c * CB + h * HC, HC), HC)
        return pltpu.make_async_copy(g.at[n, :, cols], gbuf.at[s, :, pl.ds(h * HC, HC)], g_sem.at[s, h])

    def across_cores(k):
        s = lax.rem(k, QD)
        return pltpu.make_async_remote_copy(
            dsend.at[s], drecv.at[s], ds_sem.at[s], dr_sem.at[s],
            device_id=sibling, device_id_type=MESH)

    def across_chips(k):
        s = lax.rem(k, QX)
        return pltpu.make_async_remote_copy(
            xsend.at[s], xrecv.at[s], xs_sem.at[s], xr_sem.at[s],
            device_id=partner, device_id_type=MESH)

    def place(k):
        n, r, c = where(k)
        rows = pl.ds(pl.multiple_of(r * RB + mine, HB), HB)
        cols = pl.ds(pl.multiple_of(c * CB, CB), CB)
        return res.at[n, rows, cols]

    def tail(k, group):
        own, sib = ((own1, sib1), (own2, sib2))[group]
        i = k - LATE - 1
        j = i - sum(TAILS[:group])
        src = xsend.at[lax.rem(k, QX)]
        return (
            pltpu.make_async_copy(src, own.at[j], to_sem.at[i]),
            pltpu.make_async_remote_copy(
                src, sib.at[j], ts_sem.at[i], tr_sem.at[group],
                device_id=sibling, device_id_type=MESH))

    def keep(k):
        s = lax.rem(k, QF)
        return pltpu.make_async_copy(fin.at[s], place(k), fl_sem.at[s])

    def share(k):
        s = lax.rem(k, QF)
        return pltpu.make_async_remote_copy(
            fin.at[s], place(k), fs_sem.at[s], fr_sem.at[k // (MOVES * NR)],
            device_id=sibling, device_id_type=MESH)

    late_partial = pltpu.make_async_remote_copy(
        lsend, lrecv, late_sem.at[0], late_sem.at[1], device_id=sibling, device_id_type=MESH)
    late_swap = pltpu.make_async_remote_copy(
        lsum, got0.at[0], late_sem.at[2], late_sem.at[3], device_id=partner, device_id_type=MESH)
    late_keep = pltpu.make_async_copy(lsum, own0.at[0], late_sem.at[4])
    late_share = pltpu.make_async_remote_copy(
        lsum, sib0.at[0], late_sem.at[5], late_sem.at[6], device_id=sibling, device_id_type=MESH)

    def multiply(k):
        q, r = k // NR, lax.rem(k, NR)
        n, c = q // NC, lax.rem(q, NC)
        gs = lax.rem(q, 2)

        @when(c == 0)
        def _():
            t = n * NR + r
            s = lax.rem(t, 2)
            load_a(t).wait()

            @pl.loop(0, TOK // KT)
            def _(i):
                toks = pl.ds(pl.multiple_of(i * KT, KT), KT)
                at[r, :, toks] = abuf[s, toks, :].T

            @when(t + 2 < N * NR)
            def _():
                load_a(t + 2).start()

        p = lax.rem(k, QP)

        @when(r == 0)
        def _():
            for h in range(2):
                load_g(q, h).wait()

            @when(k == 0)
            def _():
                for h in range(2):
                    load_g(1, h).start()

        prod[p] = jnp.dot(at[r], gbuf[gs], preferred_element_type=jnp.float32)

        @when((r == NR - 1) & (q + 2 < N * NC))
        def _():
            for h in range(2):
                load_g(q + 2, h).start()

        @when(k == LATE)
        def _():
            @when(core == 0)
            def _():
                lsend[...] = prod[p].astype(jnp.bfloat16)
                late_partial.start()

        @when(k != LATE)
        def _():
            s = lax.rem(k, QD)

            @when(k >= QD)
            def _():
                across_cores(k - QD).wait_send()

                @when(k != LATE + QD)
                def _():
                    pl.semaphore_wait(dfree, 1)

            dsend[s] = prod[p, pl.ds(other, HB)].astype(jnp.bfloat16)
            across_cores(k).start()

    def chip_sum(k):
        @when(k == LATE)
        def _():
            @when(core == 1)
            def _():
                late_partial.wait_recv()
                total = prod[lax.rem(k, QP)] + lrecv[...].astype(jnp.float32)
                lsum[...] = total.astype(jnp.bfloat16)
                late_swap.start()
                late_keep.start()
                late_share.start()

        @when(k != LATE)
        def _():
            own_sum(k)

    def own_sum(k):
        across_cores(k).wait_recv()
        total = prod[lax.rem(k, QP), pl.ds(mine, HB)] + drecv[lax.rem(k, QD)].astype(jnp.float32)
        xsend[lax.rem(k, QX)] = total.astype(jnp.bfloat16)

        @when((k + QD < PIECES) & (k + QD != LATE))
        def _():
            pl.semaphore_signal(dfree, inc=1, device_id=sibling, device_id_type=MESH)

        @when((k >= QX) & (k < INSIDE))
        def _():
            pl.semaphore_wait(xfree, 1)

        @when(k < INSIDE)
        def _():
            across_chips(k).start()

        for group, (lo, hi) in enumerate(GROUPS):
            @when((k >= lo) & (k < hi))
            def _():
                for copy in tail(k, group):
                    copy.start()

    def finish(k):
        across_chips(k).wait()

        @when(k >= QF)
        def _():
            keep(k - QF).wait()
            share(k - QF).wait_send()

        s = lax.rem(k, QX)
        total = xsend[s].astype(jnp.float32) + xrecv[s].astype(jnp.float32)
        fin[lax.rem(k, QF)] = total.astype(jnp.bfloat16)

        @when(k + QX < INSIDE)
        def _():
            pl.semaphore_signal(xfree, inc=1, device_id=partner, device_id_type=MESH)

        keep(k).start()
        share(k).start()

    load_a(0).start()
    load_g(0, 0).start()
    load_g(0, 1).start()
    load_a(1).start()
    barrier = pltpu.get_barrier_semaphore()
    for peer in (sibling, partner):
        pl.semaphore_signal(barrier, inc=1, device_id=peer, device_id_type=MESH)
    pl.semaphore_wait(barrier, 2)

    @pl.loop(0, INSIDE + LAG)
    def _(k):
        @when(k < PIECES)
        def _():
            multiply(k)

        @when((k != 1) & (k <= PIECES))
        def _():
            chip_sum(jnp.maximum(k - 1, 0))

        @when(k >= LAG)
        def _():
            finish(k - LAG)

    @pl.loop(PIECES - QD, PIECES)
    def _(k):
        across_cores(k).wait_send()

    @pl.loop(INSIDE - QF, INSIDE)
    def _(k):
        keep(k).wait()
        share(k).wait_send()

    for group, (lo, hi) in enumerate(GROUPS):
        @pl.loop(lo, hi)
        def _(k):
            own, sib = tail(k, group)
            own.wait()
            sib.wait_send()

        sib = (sib1, sib2)[group]
        pltpu.make_async_copy(sib, sib, tr_sem.at[group]).wait()

    whole = res.at[pl.ds(0, 2), :, pl.ds(0, MOVES * CB // 4)]
    pltpu.make_async_copy(whole, whole, fr_sem.at[0]).wait()
    rest = res.at[0, pl.ds(0, REST * HB), pl.ds(0, CB)]
    pltpu.make_async_copy(rest, rest, fr_sem.at[1]).wait()

    @when(core == 0)
    def _():
        late_partial.wait_send()
        late_share.wait_recv()

    @when(core == 1)
    def _():
        late_keep.wait()
        late_share.wait_send()
        late_swap.wait()


def move(res, out, buf, last, in_sem, out_sem, last_sem):
    def src(i):
        n, c = i // NC, lax.rem(i, NC)
        return n, slice(None), pl.ds(pl.multiple_of(c * CB, CB), CB)

    def load(i):
        s = lax.rem(i, QM)
        return pltpu.make_async_copy(res.at[src(i)], buf.at[s], in_sem.at[s])

    def store(i):
        s = lax.rem(i, QM)
        return pltpu.make_async_copy(buf.at[s], out.at[src(i)], out_sem.at[s])

    n, c = MOVES // NC, MOVES % NC
    block = (n, pl.ds(0, REST * RB), pl.ds(c * CB, CB))
    last_in = pltpu.make_async_copy(res.at[block], last, last_sem.at[0])
    last_out = pltpu.make_async_copy(last, out.at[block], last_sem.at[1])
    for i in range(QM):
        load(i).start()
    last_in.start()

    @pl.loop(0, MOVES)
    def _(i):
        load(i).wait()
        store(i).start()
        j = i - QM // 2

        @when((j >= 0) & (j + QM < MOVES))
        def _():
            store(j).wait()
            load(j + QM).start()

    last_in.wait()
    last_out.start()

    @pl.loop(MOVES - QM, MOVES)
    def _(i):
        store(i).wait()

    last_out.wait()


def settle_late(_, own, sib, got, lent, out, buf, sem):
    core = lax.rem(lax.axis_index("dp"), 2)
    n, r, c = LATE // NR // NC, LATE % NR, LATE // NR % NC
    for i, (mine, theirs) in enumerate(((sib, lent), (own, got))):
        @when(core == i)
        def _():
            total = mine[0].astype(jnp.float32) + theirs[0].astype(jnp.float32)
            buf[...] = total.astype(jnp.bfloat16)
    copy = pltpu.make_async_copy(buf, out.at[n, pl.ds(r * RB, RB), pl.ds(c * CB, CB)], sem)
    copy.start()
    copy.wait()


def settle(first, count, _, own, sib, got, lent, out, buf, sem):
    core = lax.rem(lax.axis_index("dp"), 2)
    pairs = ((core, own, got), (1 - core, sib, lent))

    def store(i, h):
        n, r, c = where(jnp.int32(first + i))
        rows = pl.ds(pl.multiple_of(r * RB + pairs[h][0] * HB, HB), HB)
        cols = pl.ds(pl.multiple_of(c * CB, CB), CB)
        return pltpu.make_async_copy(buf.at[h, i], out.at[n, rows, cols], sem.at[h, i])

    for i in range(count):
        for h, (_, mine, theirs) in enumerate(pairs):
            total = mine[i].astype(jnp.float32) + theirs[i].astype(jnp.float32)
            buf[h, i] = total.astype(jnp.bfloat16)
            store(i, h).start()
    for i in range(count):
        for h in range(2):
            store(i, h).wait()


def solution(mesh):
    dma, vmem, bf16 = pltpu.SemaphoreType.DMA, pltpu.VMEM, jnp.bfloat16
    anyspace = pl.BlockSpec(memory_space=pl.ANY)
    result = jax.ShapeDtypeStruct((N, D, FF), bf16)
    tails = [jax.ShapeDtypeStruct((t, HB, CB), bf16) for t in TAILS]
    late = jax.ShapeDtypeStruct((1, RB, CB), bf16)
    reduce = pl.pallas_call(
        kernel,
        out_shape=[result, late, *tails, late, *tails, late],
        in_specs=[anyspace, anyspace],
        out_specs=[anyspace] * 8,
        scratch_shapes=[
            vmem((NR, RB, TOK), bf16),
            vmem((2, TOK, RB), bf16),
            vmem((2, TOK, CB), bf16),
            vmem((QP, RB, CB), jnp.float32),
            vmem((QD, HB, CB), bf16),
            vmem((QD, HB, CB), bf16),
            vmem((QX, HB, CB), bf16),
            vmem((QX, HB, CB), bf16),
            vmem((QF, HB, CB), bf16),
            vmem((RB, CB), bf16), vmem((RB, CB), bf16), vmem((RB, CB), bf16),
            dma((2,)), dma((2, 2)), dma((QD,)), dma((QD,)), dma((QX,)), dma((QX,)),
            dma((QF,)), dma((QF,)), dma((2,)),
            dma((sum(TAILS),)), dma((sum(TAILS),)), dma((len(TAILS),)), dma((7,)),
            pltpu.SemaphoreType.REGULAR, pltpu.SemaphoreType.REGULAR,
        ],
        compiler_params=pltpu.CompilerParams(
            collective_id=0, has_side_effects=True, vmem_limit_bytes=60 * 2**20),
        cost_estimate=pl.CostEstimate(
            flops=2 * N * TOK * D * FF, bytes_accessed=2 * N * (TOK * (D + FF) + D * FF),
            transcendentals=0),
        name="reduce",
    )
    copy = pl.pallas_call(
        move,
        out_shape=result,
        in_specs=[anyspace],
        out_specs=anyspace,
        scratch_shapes=[
            vmem((QM, D, CB), bf16), vmem((REST * RB, CB), bf16),
            dma((QM,)), dma((QM,)), dma((2,))],
        compiler_params=pltpu.CompilerParams(vmem_limit_bytes=60 * 2**20),
        cost_estimate=pl.CostEstimate(flops=10**10, bytes_accessed=4 * N * D * FF, transcendentals=0),
        name="move",
    )

    def last(group, out, *parts):
        lo, hi = GROUPS[group]
        count = hi - lo
        return pl.pallas_call(
            functools.partial(settle, lo, count),
            out_shape=result,
            in_specs=[anyspace] + [pl.BlockSpec(memory_space=pltpu.VMEM)] * 4,
            out_specs=anyspace,
            input_output_aliases={0: 0},
            scratch_shapes=[vmem((2, count, HB, CB), bf16), dma((2, count))],
            compiler_params=pltpu.CompilerParams(vmem_limit_bytes=8 * 2**20),
            cost_estimate=pl.CostEstimate(flops=10**8, bytes_accessed=count * 2**20, transcendentals=0),
        )(out, *parts)

    def settle_first(out, *parts):
        return pl.pallas_call(
            settle_late,
            out_shape=result,
            in_specs=[anyspace] + [pl.BlockSpec(memory_space=pltpu.VMEM)] * 4,
            out_specs=anyspace,
            input_output_aliases={0: 0},
            scratch_shapes=[vmem((RB, CB), bf16), dma(())],
            compiler_params=pltpu.CompilerParams(vmem_limit_bytes=8 * 2**20),
            cost_estimate=pl.CostEstimate(flops=10**8, bytes_accessed=2**20, transcendentals=0),
            name="settle_late",
        )(out, *parts)

    swap_chips = [(i, (i + 2) % 4) for i in range(4)]
    swap_cores = [(i, i ^ 1) for i in range(4)]

    def step(a, g):
        res, own0, own1, own2, sib0, sib1, sib2, got0 = reduce(a[0], g[0])
        got1 = lax.ppermute(own1, "dp", swap_chips)
        got2 = lax.ppermute(own2, "dp", swap_chips)
        lent0 = lax.ppermute(got0, "dp", [(1, 0), (3, 2)])
        out = copy(res)
        out = settle_first(out, own0, sib0, got0, lent0)
        out, got1 = lax.optimization_barrier((out, got1))
        lent1 = lax.ppermute(got1, "dp", swap_cores)
        out = last(0, out, own1, sib1, got1, lent1)
        out, got2 = lax.optimization_barrier((out, got2))
        lent2 = lax.ppermute(got2, "dp", swap_cores)
        return last(1, out, own2, sib2, got2, lent2)

    return jax.shard_map(
        step, mesh=mesh, in_specs=(P(("rep", "dp")), P(("rep", "dp"))),
        out_specs=P("rep"), check_vma=False)
```

time: 491 us -> 469 us (0.955)
  local copies, waits for them, and re-layouts: 28.2 us -> 0.03 us
  waiting for transfers between devices: 0 us -> 19.4 us
  Pallas kernels: 463 us -> 448 us
    unnamed x1 -> x14, local copies, waits for them, and re-layouts: 28.2 us -> 0.03 us
    ppermute x0 -> x5, waiting for transfers between devices: none -> 19.4 us  [the longest x1 11.5 us: step(): got1 = lax.ppermute(own1, 'dp', swap_chips)]
    pallas_call x1 -> x5, Pallas kernels: 463 us -> 448 us  [the longest x1 418 us: step(): res, own0, own1, own2, sib0, sib1, sib2, got0 = reduce(a[0], g[0])]
  transfers between devices with their start and end apart: 0 -> 5, of which waited for: 0 -> 4; matrix products, arithmetic and copies ran while one was open for 0% -> 0% of each run, Pallas kernels for 0% -> 6%
where the time goes in v2:
time: 469 us
  Pallas kernels  448 us (96%)
  waiting for transfers between devices  19.4 us (4%)
    pallas_call x1, Pallas kernels, step(): res, own0, own1, own2, sib0, sib1, sib2, got0 = reduce(a[0], g[0])  418 us
    pallas_call x1, Pallas kernels, step(): out = copy(res)  26.1 us
    ppermute x1, waiting for transfers between devices, step(): got1 = lax.ppermute(own1, 'dp', swap_chips)  11.5 us
  transfers between devices with their start and end apart: 5, of which 4 were waited for; matrix products, arithmetic and copies ran while one was open for 0% of the time, Pallas kernels for 6%

profile of v2, /device:TPU:0, one launch (start us, length us, event | category | flops | bytes accessed | tf_op | source)
XLA Modules:
  0.0 469.3 jit_solution(2295610267439130006)
XLA Ops:
  0.0 418.4 %reduce.1 = (bf16[4,1280,4096]{2,1,0:T(8,128)(2,1)}, bf16[1,256,512]{2,1,0:T(8,128)(2,1)}, bf16[13,128,512]{2,1,0:T(8,128)(2,1)}, bf16[2,128,512]{2,1,0:T(8,128)...) custom-call(bf16[4,4096,1280]{2,1,0:T(8,128)(2,1)} %bitcast.2, ...), custom_call_target="tpu_custom_call" | custom-call | flops 171798691840 | bytes 218103808 | tf_op jit(solution)/shard_map/reduce/pallas_call | solution.py:443
  418.4 0.0 collective-permute-start.1
  418.4 1.3 collective-permute-start
  419.7 0.0 copy-start.4
  419.7 26.1 %move.1._ = bf16[4,1280,4096]{2,1,0:T(8,128)(2,1)} custom-call(bf16[4,1280,4096]{2,1,0:T(8,128)(2,1)} %get-tuple-element.17.res), custom_call_target="tpu_custom_call" | custom-call | flops 10000000000 | bytes 83886080 | tf_op jit(solution)/shard_map/move/pallas_call | solution.py:447
  445.8 0.0 collective-permute-done.lent
  445.8 0.0 copy-done.4
  445.8 0.0 copy-done.5
  445.8 0.0 copy-done.6
  445.9 0.0 copy-start.2
  445.9 0.0 copy-start
  445.9 0.0 copy-start.1
  445.9 0.8 settle_late.1._
  446.7 11.5 %collective-permute-done.1.got = bf16[13,128,512]{2,1,0:T(8,128)(2,1)S(1)} collective-permute-done((bf16[13,128,512]{2,1,0:T(8,128)(2,1)}, bf16[13,128,512]{2,1,0:T(8,128)(2,1)S(1)}, u32[]{:S(2)}, u32[]{:S(2)}) %collective-permute-start.1) | collective-permute-done | bytes 1703968 | tf_op jit(solution)/shard_map/ppermute | solution.py:444
  458.2 0.3 collective-permute-start.2
  458.5 0.0 collective-permute-start.3
  458.5 3.3 collective-permute-done.2.lent
  461.8 0.0 copy-done.1
  461.8 2.0 shard_map.28._
  463.8 3.1 collective-permute-done.3.got
  466.9 0.0 collective-permute-start.4
  466.9 1.5 collective-permute-done.4.lent
  468.5 0.0 copy-done.3
  468.5 0.9 shard_map.29
  (5 shorter events, 0.0 us)
Async XLA Ops:
  418.4 39.8 %collective-permute-start.1 = (bf16[13,128,512]{2,1,0:T(8,128)(2,1)}, bf16[13,128,512]{2,1,0:T(8,128)(2,1)S(1)}, u32[]{:S(2)}, u32[]{:S(2)}) collective-permute-start(bf16[13,128,512]{2,1,0:T(8,128)(2,1)} %get-tuple-element.21.own), channel_id=1, source_target_pairs={{0,2},{1,3},{2,0},{3,1},{4,6},{5,7},{6,4},{7,5}} | collective-permute-start | bytes 5111816 | tf_op jit(solution)/shard_map/ppermute | solution.py:444
  418.4 27.4 %collective-permute-start = (bf16[1,256,512]{2,1,0:T(8,128)(2,1)}, bf16[1,256,512]{2,1,0:T(8,128)(2,1)S(1)}, u32[]{:S(2)}, u32[]{:S(2)}) collective-permute-start(bf16[1,256,512]{2,1,0:T(8,128)(2,1)} %get-tuple-element.20.got), channel_id=1, source_target_pairs={{1,0},{3,2},{5,4},{7,6}} | collective-permute-start | bytes 786440 | tf_op jit(solution)/shard_map/ppermute | solution.py:446
  419.7 26.1 %copy-start.4 = (bf16[1,256,512]{2,1,0:T(8,128)(2,1)S(1)}, bf16[1,256,512]{2,1,0:T(8,128)(2,1)}, u32[]{:S(2)}) copy-start(bf16[1,256,512]{2,1,0:T(8,128)(2,1)} %get-tuple-element.18.own) | copy-start | bytes 786436
  419.7 26.1 %copy-start.5 = (bf16[1,256,512]{2,1,0:T(8,128)(2,1)S(1)}, bf16[1,256,512]{2,1,0:T(8,128)(2,1)}, u32[]{:S(2)}) copy-start(bf16[1,256,512]{2,1,0:T(8,128)(2,1)} %get-tuple-element.19.sib) | copy-start | bytes 786436
  419.7 26.1 %copy-start.6 = (bf16[1,256,512]{2,1,0:T(8,128)(2,1)S(1)}, bf16[1,256,512]{2,1,0:T(8,128)(2,1)}, u32[]{:S(2)}) copy-start(bf16[1,256,512]{2,1,0:T(8,128)(2,1)} %get-tuple-element.20.got) | copy-start | bytes 786436
  445.9 12.7 %copy-start.2 = (bf16[2,128,512]{2,1,0:T(8,128)(2,1)S(1)}, bf16[2,128,512]{2,1,0:T(8,128)(2,1)}, u32[]{:S(2)}) copy-start(bf16[2,128,512]{2,1,0:T(8,128)(2,1)} %get-tuple-element.25.own) | copy-start | bytes 786436
  445.9 15.9 %copy-start = (bf16[13,128,512]{2,1,0:T(8,128)(2,1)S(1)}, bf16[13,128,512]{2,1,0:T(8,128)(2,1)}, u32[]{:S(2)}) copy-start(bf16[13,128,512]{2,1,0:T(8,128)(2,1)} %get-tuple-element.21.own) | copy-start | bytes 5111812
  445.9 15.9 %copy-start.1 = (bf16[13,128,512]{2,1,0:T(8,128)(2,1)S(1)}, bf16[13,128,512]{2,1,0:T(8,128)(2,1)}, u32[]{:S(2)}) copy-start(bf16[13,128,512]{2,1,0:T(8,128)(2,1)} %get-tuple-element.23.sib) | copy-start | bytes 5111812
  458.2 3.6 collective-permute-start.2
  458.5 8.4 %collective-permute-start.3 = (bf16[2,128,512]{2,1,0:T(8,128)(2,1)S(1)}, bf16[2,128,512]{2,1,0:T(8,128)(2,1)S(1)}, u32[]{:S(2)}, u32[]{:S(2)}) collective-permute-start(bf16[2,128,512]{2,1,0:T(8,128)(2,1)S(1)} %copy-done.2), channel_id=1, source_target_pairs={{0,2},{1,3},{2,0},{3,1},{4,6},{5,7},{6,4},{7,5}} | collective-permute-start | bytes 786440 | tf_op jit(solution)/shard_map/ppermute | solution.py:445
  461.8 6.7 %copy-start.3 = (bf16[2,128,512]{2,1,0:T(8,128)(2,1)S(1)}, bf16[2,128,512]{2,1,0:T(8,128)(2,1)}, u32[]{:S(2)}) copy-start(bf16[2,128,512]{2,1,0:T(8,128)(2,1)} %get-tuple-element.27.sib) | copy-start | bytes 786436
  466.9 1.5 collective-permute-start.4

commit v3 on v2

--- a/solution.py
+++ b/solution.py
@@ -15,9 +15,10 @@
 HB = RB // 2
 NR, NC = D // RB, FF // CB
 PIECES = N * NC * NR
-TAILS = (13, 2)
-LATE = PIECES - sum(TAILS) - 1
-INSIDE = LATE
+TAILS = (8, 5, 2)
+LATES = 2
+INSIDE = PIECES - sum(TAILS) - LATES
+AFTER = INSIDE + LATES
 KT = 512
 LAG = 24
 QX = LAG + 2
@@ -40,9 +41,12 @@
     return q // NC, lax.rem(k, NR), lax.rem(q, NC)
 
 
-def kernel(a, g, res, own0, own1, own2, sib0, sib1, sib2, got0, at, abuf, gbuf, prod, dsend, drecv, xsend, xrecv, fin, lsend, lrecv, lsum,
-           a_sem, g_sem, ds_sem, dr_sem, xs_sem, xr_sem, fl_sem, fs_sem, fr_sem,
-           to_sem, ts_sem, tr_sem, late_sem, dfree, xfree):
+def kernel(a, g, res, own0, sib0, got0, *refs):
+    n = len(TAILS)
+    owns, sibs = refs[:n], refs[n:2 * n]
+    (at, abuf, gbuf, prod, dsend, drecv, xsend, xrecv, fin, lsend, lrecv, lsum,
+     a_sem, g_sem, ds_sem, dr_sem, xs_sem, xr_sem, fl_sem, fs_sem, fr_sem,
+     to_sem, ts_sem, tr_sem, late_sem, early_sem, dfree, xfree) = refs[2 * n:]
     rep, me = lax.axis_index("rep"), lax.axis_index("dp")
     core = lax.rem(me, 2)
     sibling = (rep, me + 1 - 2 * core)
@@ -81,14 +85,13 @@
         return res.at[n, rows, cols]
 
     def tail(k, group):
-        own, sib = ((own1, sib1), (own2, sib2))[group]
-        i = k - LATE - 1
+        i = k - AFTER
         j = i - sum(TAILS[:group])
         src = xsend.at[lax.rem(k, QX)]
         return (
-            pltpu.make_async_copy(src, own.at[j], to_sem.at[i]),
+            pltpu.make_async_copy(src, owns[group].at[j], to_sem.at[i]),
             pltpu.make_async_remote_copy(
-                src, sib.at[j], ts_sem.at[i], tr_sem.at[group],
+                src, sibs[group].at[j], ts_sem.at[i], tr_sem.at[group],
                 device_id=sibling, device_id_type=MESH))
 
     def keep(k):
@@ -101,13 +104,78 @@
             fin.at[s], place(k), fs_sem.at[s], fr_sem.at[k // (MOVES * NR)],
             device_id=sibling, device_id_type=MESH)
 
-    late_partial = pltpu.make_async_remote_copy(
-        lsend, lrecv, late_sem.at[0], late_sem.at[1], device_id=sibling, device_id_type=MESH)
-    late_swap = pltpu.make_async_remote_copy(
-        lsum, got0.at[0], late_sem.at[2], late_sem.at[3], device_id=partner, device_id_type=MESH)
-    late_keep = pltpu.make_async_copy(lsum, own0.at[0], late_sem.at[4])
-    late_share = pltpu.make_async_remote_copy(
-        lsum, sib0.at[0], late_sem.at[5], late_sem.at[6], device_id=sibling, device_id_type=MESH)
+    def late_partial(i):
+        return pltpu.make_async_remote_copy(
+            lsend.at[i], lrecv.at[i], late_sem.at[i, 0], late_sem.at[i, 1],
+            device_id=sibling, device_id_type=MESH)
+
+    def late_swap(i):
+        return pltpu.make_async_remote_copy(
+            lsum.at[i], got0.at[i], late_sem.at[i, 2], late_sem.at[i, 3],
+            device_id=partner, device_id_type=MESH)
+
+    def late_keep(i):
+        return pltpu.make_async_copy(lsum.at[i], own0.at[i], late_sem.at[i, 4])
+
+    def late_share(i):
+        return pltpu.make_async_remote_copy(
+            lsum.at[i], sib0.at[i], late_sem.at[i, 5], late_sem.at[i, 6],
+            device_id=sibling, device_id_type=MESH)
+
+    def is_late(k):
+        return (k >= INSIDE) & (k < AFTER)
+
+    def turn(t):
+        s, r = lax.rem(t, 2), lax.rem(t, NR)
+
+        @pl.loop(0, TOK // KT)
+        def _(i):
+            toks = pl.ds(pl.multiple_of(i * KT, KT), KT)
+            at[r, :, toks] = abuf[s, toks, :].T
+
+        @when(t + 2 < N * NR)
+        def _():
+            load_a(t + 2).start()
+
+    def first_piece():
+        def part(ref, h, rows=slice(None)):
+            return ref.at[0, rows, pl.ds(h * HC, HC)]
+
+        def partial(h):
+            return pltpu.make_async_remote_copy(
+                part(dsend, h), part(drecv, h), ds_sem.at[0], early_sem.at[h],
+                device_id=sibling, device_id_type=MESH)
+
+        def swap(h):
+            return pltpu.make_async_remote_copy(
+                part(xsend, h), part(xrecv, h), xs_sem.at[0], xr_sem.at[0],
+                device_id=partner, device_id_type=MESH)
+
+        load_a(0).wait()
+        load_g(0, 1).start()
+        load_a(1).start()
+        turn(jnp.int32(0))
+        for h in range(2):
+            load_g(0, h).wait()
+            part(prod, h)[...] = jnp.dot(
+                at[0], part(gbuf, h)[...], preferred_element_type=jnp.float32)
+            part(dsend, h)[...] = part(prod, h, pl.ds(other, HB))[...].astype(jnp.bfloat16)
+            partial(h).start()
+        for h in range(2):
+            load_g(1, h).start()
+        for h in range(2):
+            partial(h).wait_recv()
+            total = part(prod, h, pl.ds(mine, HB))[...] + part(drecv, h)[...].astype(jnp.float32)
+            part(xsend, h)[...] = total.astype(jnp.bfloat16)
+            swap(h).start()
+        pl.semaphore_signal(dfree, inc=1, device_id=sibling, device_id_type=MESH)
+
+    def first_sum(k):
+        across_cores(k).wait_recv()
+        total = prod[lax.rem(k, QP), pl.ds(mine, HB)] + drecv[lax.rem(k, QD)].astype(jnp.float32)
+        xsend[k] = total.astype(jnp.bfloat16)
+        pl.semaphore_signal(dfree, inc=1, device_id=sibling, device_id_type=MESH)
+        across_chips(k).start()
 
     def multiply(k):
         q, r = k // NR, lax.rem(k, NR)
@@ -116,31 +184,19 @@
 
         @when(c == 0)
         def _():
-            t = n * NR + r
-            s = lax.rem(t, 2)
-            load_a(t).wait()
-
-            @pl.loop(0, TOK // KT)
-            def _(i):
-                toks = pl.ds(pl.multiple_of(i * KT, KT), KT)
-                at[r, :, toks] = abuf[s, toks, :].T
-
-            @when(t + 2 < N * NR)
-            def _():
-                load_a(t + 2).start()
-
-        p = lax.rem(k, QP)
+            load_a(n * NR + r).wait()
+            turn(n * NR + r)
+
+        @when((k >= 2) & (k <= NR))
+        def _():
+            first_sum(k - 1)
 
         @when(r == 0)
         def _():
             for h in range(2):
                 load_g(q, h).wait()
 
-            @when(k == 0)
-            def _():
-                for h in range(2):
-                    load_g(1, h).start()
-
+        p = lax.rem(k, QP)
         prod[p] = jnp.dot(at[r], gbuf[gs], preferred_element_type=jnp.float32)
 
         @when((r == NR - 1) & (q + 2 < N * NC))
@@ -148,14 +204,12 @@
             for h in range(2):
                 load_g(q + 2, h).start()
 
-        @when(k == LATE)
-        def _():
-            @when(core == 0)
-            def _():
-                lsend[...] = prod[p].astype(jnp.bfloat16)
-                late_partial.start()
-
-        @when(k != LATE)
+        @when(is_late(k) & (core == 0))
+        def _():
+            lsend[k - INSIDE] = prod[p].astype(jnp.bfloat16)
+            late_partial(k - INSIDE).start()
+
+        @when(~is_late(k))
         def _():
             s = lax.rem(k, QD)
 
@@ -163,7 +217,7 @@
             def _():
                 across_cores(k - QD).wait_send()
 
-                @when(k != LATE + QD)
+                @when(~is_late(k - QD))
                 def _():
                     pl.semaphore_wait(dfree, 1)
 
@@ -171,18 +225,17 @@
             across_cores(k).start()
 
     def chip_sum(k):
-        @when(k == LATE)
-        def _():
-            @when(core == 1)
-            def _():
-                late_partial.wait_recv()
-                total = prod[lax.rem(k, QP)] + lrecv[...].astype(jnp.float32)
-                lsum[...] = total.astype(jnp.bfloat16)
-                late_swap.start()
-                late_keep.start()
-                late_share.start()
-
-        @when(k != LATE)
+        @when(is_late(k) & (core == 1))
+        def _():
+            i = k - INSIDE
+            late_partial(i).wait_recv()
+            total = prod[lax.rem(k, QP)] + lrecv[i].astype(jnp.float32)
+            lsum[i] = total.astype(jnp.bfloat16)
+            late_swap(i).start()
+            late_keep(i).start()
+            late_share(i).start()
+
+        @when(~is_late(k))
         def _():
             own_sum(k)
 
@@ -191,7 +244,7 @@
         total = prod[lax.rem(k, QP), pl.ds(mine, HB)] + drecv[lax.rem(k, QD)].astype(jnp.float32)
         xsend[lax.rem(k, QX)] = total.astype(jnp.bfloat16)
 
-        @when((k + QD < PIECES) & (k + QD != LATE))
+        @when((k + QD < PIECES) & ~is_late(k + QD))
         def _():
             pl.semaphore_signal(dfree, inc=1, device_id=sibling, device_id_type=MESH)
 
@@ -230,22 +283,22 @@
 
     load_a(0).start()
     load_g(0, 0).start()
-    load_g(0, 1).start()
-    load_a(1).start()
     barrier = pltpu.get_barrier_semaphore()
     for peer in (sibling, partner):
         pl.semaphore_signal(barrier, inc=1, device_id=peer, device_id_type=MESH)
     pl.semaphore_wait(barrier, 2)
 
-    @pl.loop(0, INSIDE + LAG)
+    first_piece()
+
+    @pl.loop(1, INSIDE + LAG)
     def _(k):
         @when(k < PIECES)
         def _():
             multiply(k)
 
-        @when((k != 1) & (k <= PIECES))
-        def _():
-            chip_sum(jnp.maximum(k - 1, 0))
+        @when((k > NR) & (k <= PIECES))
+        def _():
+            chip_sum(k - 1)
 
         @when(k >= LAG)
         def _():
@@ -267,7 +320,7 @@
             own.wait()
             sib.wait_send()
 
-        sib = (sib1, sib2)[group]
+        sib = sibs[group]
         pltpu.make_async_copy(sib, sib, tr_sem.at[group]).wait()
 
     whole = res.at[pl.ds(0, 2), :, pl.ds(0, MOVES * CB // 4)]
@@ -277,14 +330,16 @@
 
     @when(core == 0)
     def _():
-        late_partial.wait_send()
-        late_share.wait_recv()
+        for i in range(LATES):
+            late_partial(i).wait_send()
+            late_share(i).wait_recv()
 
     @when(core == 1)
     def _():
-        late_keep.wait()
-        late_share.wait_send()
-        late_swap.wait()
+        for i in range(LATES):
+            late_keep(i).wait()
+            late_share(i).wait_send()
+            late_swap(i).wait()
 
 
 def move(res, out, buf, last, in_sem, out_sem, last_sem):
@@ -331,15 +386,22 @@
 
 def settle_late(_, own, sib, got, lent, out, buf, sem):
     core = lax.rem(lax.axis_index("dp"), 2)
-    n, r, c = LATE // NR // NC, LATE % NR, LATE // NR % NC
     for i, (mine, theirs) in enumerate(((sib, lent), (own, got))):
         @when(core == i)
         def _():
-            total = mine[0].astype(jnp.float32) + theirs[0].astype(jnp.float32)
-            buf[...] = total.astype(jnp.bfloat16)
-    copy = pltpu.make_async_copy(buf, out.at[n, pl.ds(r * RB, RB), pl.ds(c * CB, CB)], sem)
-    copy.start()
-    copy.wait()
+            for j in range(LATES):
+                total = mine[j].astype(jnp.float32) + theirs[j].astype(jnp.float32)
+                buf[j] = total.astype(jnp.bfloat16)
+    copies = []
+    for j in range(LATES):
+        n, r, c = where(jnp.int32(INSIDE + j))
+        rows = pl.ds(pl.multiple_of(r * RB, RB), RB)
+        cols = pl.ds(pl.multiple_of(c * CB, CB), CB)
+        copies.append(pltpu.make_async_copy(buf.at[j], out.at[n, rows, cols], sem.at[j]))
+    for copy in copies:
+        copy.start()
+    for copy in copies:
+        copy.wait()
 
 
 def settle(first, count, _, own, sib, got, lent, out, buf, sem):
@@ -367,12 +429,12 @@
     anyspace = pl.BlockSpec(memory_space=pl.ANY)
     result = jax.ShapeDtypeStruct((N, D, FF), bf16)
     tails = [jax.ShapeDtypeStruct((t, HB, CB), bf16) for t in TAILS]
-    late = jax.ShapeDtypeStruct((1, RB, CB), bf16)
+    late = jax.ShapeDtypeStruct((LATES, RB, CB), bf16)
     reduce = pl.pallas_call(
         kernel,
-        out_shape=[result, late, *tails, late, *tails, late],
+        out_shape=[result, late, late, late, *tails, *tails],
         in_specs=[anyspace, anyspace],
-        out_specs=[anyspace] * 8,
+        out_specs=[anyspace] * (4 + 2 * len(TAILS)),
         scratch_shapes=[
             vmem((NR, RB, TOK), bf16),
             vmem((2, TOK, RB), bf16),
@@ -383,10 +445,10 @@
             vmem((QX, HB, CB), bf16),
             vmem((QX, HB, CB), bf16),
             vmem((QF, HB, CB), bf16),
-            vmem((RB, CB), bf16), vmem((RB, CB), bf16), vmem((RB, CB), bf16),
+            *[vmem((LATES, RB, CB), bf16)] * 3,
             dma((2,)), dma((2, 2)), dma((QD,)), dma((QD,)), dma((QX,)), dma((QX,)),
             dma((QF,)), dma((QF,)), dma((2,)),
-            dma((sum(TAILS),)), dma((sum(TAILS),)), dma((len(TAILS),)), dma((7,)),
+            dma((sum(TAILS),)), dma((sum(TAILS),)), dma((len(TAILS),)), dma((LATES, 7)), dma((2,)),
             pltpu.SemaphoreType.REGULAR, pltpu.SemaphoreType.REGULAR,
         ],
         compiler_params=pltpu.CompilerParams(
@@ -430,7 +492,7 @@
             in_specs=[anyspace] + [pl.BlockSpec(memory_space=pltpu.VMEM)] * 4,
             out_specs=anyspace,
             input_output_aliases={0: 0},
-            scratch_shapes=[vmem((RB, CB), bf16), dma(())],
+            scratch_shapes=[vmem((LATES, RB, CB), bf16), dma((LATES,))],
             compiler_params=pltpu.CompilerParams(vmem_limit_bytes=8 * 2**20),
             cost_estimate=pl.CostEstimate(flops=10**8, bytes_accessed=2**20, transcendentals=0),
             name="settle_late",
@@ -440,18 +502,19 @@
     swap_cores = [(i, i ^ 1) for i in range(4)]
 
     def step(a, g):
-        res, own0, own1, own2, sib0, sib1, sib2, got0 = reduce(a[0], g[0])
-        got1 = lax.ppermute(own1, "dp", swap_chips)
-        got2 = lax.ppermute(own2, "dp", swap_chips)
+        res, own0, sib0, got0, *tail = reduce(a[0], g[0])
+        owns, sibs = tail[:len(TAILS)], tail[len(TAILS):]
+        gots = []
+        for own in owns:
+            gots.append(lax.ppermute(own, "dp", swap_chips))
         lent0 = lax.ppermute(got0, "dp", [(1, 0), (3, 2)])
         out = copy(res)
         out = settle_first(out, own0, sib0, got0, lent0)
-        out, got1 = lax.optimization_barrier((out, got1))
-        lent1 = lax.ppermute(got1, "dp", swap_cores)
-        out = last(0, out, own1, sib1, got1, lent1)
-        out, got2 = lax.optimization_barrier((out, got2))
-        lent2 = lax.ppermute(got2, "dp", swap_cores)
-        return last(1, out, own2, sib2, got2, lent2)
+        for i, (own, sib, got) in enumerate(zip(owns, sibs, gots)):
+            out, got = lax.optimization_barrier((out, got))
+            lent = lax.ppermute(got, "dp", swap_cores)
+            out = last(i, out, own, sib, got, lent)
+        return out
 
     return jax.shard_map(
         step, mesh=mesh, in_specs=(P(("rep", "dp")), P(("rep", "dp"))),

time: 469 us -> 476 us (1.015)
  starting transfers between devices: 1.64 us -> 8.56 us
    ppermute x4 -> x6, starting transfers between devices: 0.35 us -> 7.28 us  [the longest x3 3.65 us: step(): lent = lax.ppermute(got, 'dp', swap_cores)]
    ppermute x4 -> x6, waiting for transfers between devices: 19.4 us -> 21.1 us  [the longest x3 18.4 us: step(): gots.append(lax.ppermute(own, 'dp', swap_chips))]
  transfers between devices with their start and end apart: 5 -> 7, of which waited for: 4 -> 5; matrix products, arithmetic and copies ran while one was open for 0% -> 0% of each run, Pallas kernels for 6% -> 6%
where the time goes in v3:
time: 476 us
  Pallas kernels  446 us (94%)
  waiting for transfers between devices  21.1 us (4%)
  starting transfers between devices  8.56 us (2%)
    pallas_call x1, Pallas kernels, step(): res, own0, sib0, got0, *tail = reduce(a[0], g[0])  416 us
    pallas_call x1, Pallas kernels, step(): out = copy(res)  26.4 us
    ppermute x3, waiting for transfers between devices, step(): gots.append(lax.ppermute(own, 'dp', swap_chips))  18.4 us
  transfers between devices with their start and end apart: 7, of which 5 were waited for; matrix products, arithmetic and copies ran while one was open for 0% of the time, Pallas kernels for 6%

profile of v3, /device:TPU:0, one launch (start us, length us, event | category | flops | bytes accessed | tf_op | source)
XLA Modules:
  0.0 476.4 jit_solution(9678562681217245168)
XLA Ops:
  0.0 415.6 %reduce.1 = (bf16[4,1280,4096]{2,1,0:T(8,128)(2,1)}, bf16[2,256,512]{2,1,0:T(8,128)(2,1)}, bf16[2,256,512]{2,1,0:T(8,128)(2,1)}, bf16[2,256,512]{2,1,0:T(8,128)(...) custom-call(bf16[4,4096,1280]{2,1,0:T(8,128)(2,1)} %bitcast.2, ...), custom_call_target="tpu_custom_call" | custom-call | flops 171798691840 | bytes 218103808 | tf_op jit(solution)/shard_map/reduce/pallas_call | solution.py:505
  415.6 0.5 collective-permute-start.1
  416.1 1.3 collective-permute-start
  417.4 26.4 %move.1._ = bf16[4,1280,4096]{2,1,0:T(8,128)(2,1)} custom-call(bf16[4,1280,4096]{2,1,0:T(8,128)(2,1)} %get-tuple-element.21.res), custom_call_target="tpu_custom_call" | custom-call | flops 10000000000 | bytes 83886080 | tf_op jit(solution)/shard_map/move/pallas_call | solution.py:511
  443.8 0.0 collective-permute-done.lent
  443.9 0.0 copy-done.4
  443.9 0.0 copy-done.5
  443.9 0.0 copy-done.6
  443.9 0.0 copy-start.2
  443.9 0.9 settle_late.1._
  444.9 0.0 collective-permute-done.1.got
  444.9 3.6 collective-permute-start.2
  448.5 1.6 collective-permute-start.3
  450.1 0.7 collective-permute-done.2.lent
  450.8 1.5 shard_map.28._
  452.3 13.0 %collective-permute-done.3.got = bf16[5,128,512]{2,1,0:T(8,128)(2,1)S(1)} collective-permute-done((bf16[5,128,512]{2,1,0:T(8,128)(2,1)S(1)}, bf16[5,128,512]{2,1,0:T(8,128)(2,1)S(1)}, u32[]{:S(2)}, u32[]{:S(2)}) %collective-permute-start.3) | collective-permute-done | bytes 655392 | tf_op jit(solution)/shard_map/ppermute | solution.py:509
  465.3 0.0 collective-permute-start.4
  465.3 1.6 collective-permute-start.5
  466.9 0.5 collective-permute-done.4.lent
  467.4 1.2 shard_map.29._
  468.5 5.5 %collective-permute-done.5.got = bf16[2,128,512]{2,1,0:T(8,128)(2,1)S(1)} collective-permute-done((bf16[2,128,512]{2,1,0:T(8,128)(2,1)S(1)}, bf16[2,128,512]{2,1,0:T(8,128)(2,1)S(1)}, u32[]{:S(2)}, u32[]{:S(2)}) %collective-permute-start.5) | collective-permute-done | bytes 262176 | tf_op jit(solution)/shard_map/ppermute | solution.py:509
  474.0 0.0 collective-permute-start.6
  474.0 1.5 collective-permute-done.6.lent
  475.5 0.9 shard_map.30
  (14 shorter events, 0.0 us)
Async XLA Ops:
  415.6 29.2 %collective-permute-start.1 = (bf16[8,128,512]{2,1,0:T(8,128)(2,1)}, bf16[8,128,512]{2,1,0:T(8,128)(2,1)S(1)}, u32[]{:S(2)}, u32[]{:S(2)}) collective-permute-start(bf16[8,128,512]{2,1,0:T(8,128)(2,1)} %get-tuple-element.25.own), channel_id=1, source_target_pairs={{0,2},{1,3},{2,0},{3,1},{4,6},{5,7},{6,4},{7,5}} | collective-permute-start | bytes 3145736 | tf_op jit(solution)/shard_map/ppermute | solution.py:509
  416.1 27.8 %collective-permute-start = (bf16[2,256,512]{2,1,0:T(8,128)(2,1)}, bf16[2,256,512]{2,1,0:T(8,128)(2,1)S(1)}, u32[]{:S(2)}, u32[]{:S(2)}) collective-permute-start(bf16[2,256,512]{2,1,0:T(8,128)(2,1)} %get-tuple-element.24.got), channel_id=1, source_target_pairs={{1,0},{3,2},{5,4},{7,6}} | collective-permute-start | bytes 1572872 | tf_op jit(solution)/shard_map/ppermute | solution.py:510
  417.4 26.5 %copy-start.4 = (bf16[2,256,512]{2,1,0:T(8,128)(2,1)S(1)}, bf16[2,256,512]{2,1,0:T(8,128)(2,1)}, u32[]{:S(2)}) copy-start(bf16[2,256,512]{2,1,0:T(8,128)(2,1)} %get-tuple-element.22.own) | copy-start | bytes 1572868
  417.4 26.5 %copy-start.5 = (bf16[2,256,512]{2,1,0:T(8,128)(2,1)S(1)}, bf16[2,256,512]{2,1,0:T(8,128)(2,1)}, u32[]{:S(2)}) copy-start(bf16[2,256,512]{2,1,0:T(8,128)(2,1)} %get-tuple-element.23.sib) | copy-start | bytes 1572868
  417.4 26.5 %copy-start.6 = (bf16[2,256,512]{2,1,0:T(8,128)(2,1)S(1)}, bf16[2,256,512]{2,1,0:T(8,128)(2,1)}, u32[]{:S(2)}) copy-start(bf16[2,256,512]{2,1,0:T(8,128)(2,1)} %get-tuple-element.24.got) | copy-start | bytes 1572868
  443.9 4.6 copy-start.2
  443.9 6.9 %copy-start = (bf16[8,128,512]{2,1,0:T(8,128)(2,1)S(1)}, bf16[8,128,512]{2,1,0:T(8,128)(2,1)}, u32[]{:S(2)}) copy-start(bf16[8,128,512]{2,1,0:T(8,128)(2,1)} %get-tuple-element.25.own) | copy-start | bytes 3145732
  443.9 6.9 %copy-start.1 = (bf16[8,128,512]{2,1,0:T(8,128)(2,1)S(1)}, bf16[8,128,512]{2,1,0:T(8,128)(2,1)}, u32[]{:S(2)}) copy-start(bf16[8,128,512]{2,1,0:T(8,128)(2,1)} %get-tuple-element.27.sib) | copy-start | bytes 3145732
  444.9 5.9 %collective-permute-start.2 = (bf16[8,128,512]{2,1,0:T(8,128)(2,1)S(1)}, bf16[8,128,512]{2,1,0:T(8,128)(2,1)S(1)}, u32[]{:S(2)}, u32[]{:S(2)}) collective-permute-start(bf16[8,128,512]{2,1,0:T(8,128)(2,1)S(1)} %collective-permute-done.1.got), channel_id=1, source_target_pairs={{0,1},{1,0},{2,3},{3,2},{4,5},{5,4},{6,7},{7,6}} | collective-permute-start | bytes 3145736 | tf_op jit(solution)/shard_map/ppermute | solution.py:515
  448.5 16.7 %collective-permute-start.3 = (bf16[5,128,512]{2,1,0:T(8,128)(2,1)S(1)}, bf16[5,128,512]{2,1,0:T(8,128)(2,1)S(1)}, u32[]{:S(2)}, u32[]{:S(2)}) collective-permute-start(bf16[5,128,512]{2,1,0:T(8,128)(2,1)S(1)} %copy-done.2), channel_id=1, source_target_pairs={{0,2},{1,3},{2,0},{3,1},{4,6},{5,7},{6,4},{7,5}} | collective-permute-start | bytes 1966088 | tf_op jit(solution)/shard_map/ppermute | solution.py:509
  450.8 14.4 %copy-start.7 = (bf16[2,128,512]{2,1,0:T(8,128)(2,1)S(1)}, bf16[2,128,512]{2,1,0:T(8,128)(2,1)}, u32[]{:S(2)}) copy-start(bf16[2,128,512]{2,1,0:T(8,128)(2,1)} %get-tuple-element.33.own) | copy-start | bytes 786436
  450.8 16.5 %copy-start.3 = (bf16[5,128,512]{2,1,0:T(8,128)(2,1)S(1)}, bf16[5,128,512]{2,1,0:T(8,128)(2,1)}, u32[]{:S(2)}) copy-start(bf16[5,128,512]{2,1,0:T(8,128)(2,1)} %get-tuple-element.31.sib) | copy-start | bytes 1966084
  465.3 2.1 collective-permute-start.4
  465.3 8.7 %collective-permute-start.5 = (bf16[2,128,512]{2,1,0:T(8,128)(2,1)S(1)}, bf16[2,128,512]{2,1,0:T(8,128)(2,1)S(1)}, u32[]{:S(2)}, u32[]{:S(2)}) collective-permute-start(bf16[2,128,512]{2,1,0:T(8,128)(2,1)S(1)} %copy-done.7), channel_id=1, source_target_pairs={{0,2},{1,3},{2,0},{3,1},{4,6},{5,7},{6,4},{7,5}} | collective-permute-start | bytes 786440 | tf_op jit(solution)/shard_map/ppermute | solution.py:509
  467.4 8.2 %copy-start.8 = (bf16[2,128,512]{2,1,0:T(8,128)(2,1)S(1)}, bf16[2,128,512]{2,1,0:T(8,128)(2,1)}, u32[]{:S(2)}) copy-start(bf16[2,128,512]{2,1,0:T(8,128)(2,1)} %get-tuple-element.35.sib) | copy-start | bytes 786436
  474.0 1.5 collective-permute-start.6

commit v4 on v3

--- a/solution.py
+++ b/solution.py
@@ -24,6 +24,7 @@
 QX = LAG + 2
 QD = 4
 QP = 3
+FIRST = 1
 QF = 4
 
 
@@ -137,32 +138,32 @@
         def _():
             load_a(t + 2).start()
 
-    def first_piece():
-        def part(ref, h, rows=slice(None)):
-            return ref.at[0, rows, pl.ds(h * HC, HC)]
+    def first_piece(k):
+        def part(ref, h, rows=slice(None), slot=k):
+            return ref.at[slot, rows, pl.ds(h * HC, HC)]
 
         def partial(h):
             return pltpu.make_async_remote_copy(
-                part(dsend, h), part(drecv, h), ds_sem.at[0], early_sem.at[h],
+                part(dsend, h), part(drecv, h), ds_sem.at[k], early_sem.at[k, h],
                 device_id=sibling, device_id_type=MESH)
 
         def swap(h):
             return pltpu.make_async_remote_copy(
-                part(xsend, h), part(xrecv, h), xs_sem.at[0], xr_sem.at[0],
+                part(xsend, h), part(xrecv, h), xs_sem.at[k], xr_sem.at[k],
                 device_id=partner, device_id_type=MESH)
 
-        load_a(0).wait()
-        load_g(0, 1).start()
-        load_a(1).start()
-        turn(jnp.int32(0))
         for h in range(2):
-            load_g(0, h).wait()
+            if k == 0:
+                load_g(0, h).wait()
             part(prod, h)[...] = jnp.dot(
-                at[0], part(gbuf, h)[...], preferred_element_type=jnp.float32)
+                at[k], part(gbuf, h, slot=0)[...], preferred_element_type=jnp.float32)
             part(dsend, h)[...] = part(prod, h, pl.ds(other, HB))[...].astype(jnp.bfloat16)
             partial(h).start()
-        for h in range(2):
-            load_g(1, h).start()
+        load_a(k + 1).wait()
+        turn(jnp.int32(k + 1))
+        if k == 0:
+            for h in range(2):
+                load_g(1, h).start()
         for h in range(2):
             partial(h).wait_recv()
             total = part(prod, h, pl.ds(mine, HB))[...] + part(drecv, h)[...].astype(jnp.float32)
@@ -182,12 +183,12 @@
         n, c = q // NC, lax.rem(q, NC)
         gs = lax.rem(q, 2)
 
-        @when(c == 0)
+        @when((c == 0) & (k > FIRST))
         def _():
             load_a(n * NR + r).wait()
             turn(n * NR + r)
 
-        @when((k >= 2) & (k <= NR))
+        @when((k > FIRST) & (k <= NR))
         def _():
             first_sum(k - 1)
 
@@ -288,9 +289,14 @@
         pl.semaphore_signal(barrier, inc=1, device_id=peer, device_id_type=MESH)
     pl.semaphore_wait(barrier, 2)
 
-    first_piece()
-
-    @pl.loop(1, INSIDE + LAG)
+    load_a(0).wait()
+    load_g(0, 1).start()
+    load_a(1).start()
+    turn(jnp.int32(0))
+    for k in range(FIRST):
+        first_piece(k)
+
+    @pl.loop(FIRST, INSIDE + LAG)
     def _(k):
         @when(k < PIECES)
         def _():
@@ -448,7 +454,7 @@
             *[vmem((LATES, RB, CB), bf16)] * 3,
             dma((2,)), dma((2, 2)), dma((QD,)), dma((QD,)), dma((QX,)), dma((QX,)),
             dma((QF,)), dma((QF,)), dma((2,)),
-            dma((sum(TAILS),)), dma((sum(TAILS),)), dma((len(TAILS),)), dma((LATES, 7)), dma((2,)),
+            dma((sum(TAILS),)), dma((sum(TAILS),)), dma((len(TAILS),)), dma((LATES, 7)), dma((FIRST, 2)),
             pltpu.SemaphoreType.REGULAR, pltpu.SemaphoreType.REGULAR,
         ],
         compiler_params=pltpu.CompilerParams(

time: 476 us -> 476 us (level)
  no operation moved by 1% of the time
where the time goes in v4:
time: 476 us; the launch traced here: 475 us
  Pallas kernels  446 us (94%)
  waiting for transfers between devices  21.1 us (4%)
  starting transfers between devices  8.55 us (2%)
    pallas_call x1, Pallas kernels, step(): res, own0, sib0, got0, *tail = reduce(a[0], g[0])  415 us
    pallas_call x1, Pallas kernels, step(): out = copy(res)  26.4 us
    ppermute x3, waiting for transfers between devices, step(): gots.append(lax.ppermute(own, 'dp', swap_chips))  18.4 us
  transfers between devices with their start and end apart: 7, of which 5 were waited for; matrix products, arithmetic and copies ran while one was open for 0% of the time, Pallas kernels for 6%

profile of v4, /device:TPU:0, one launch (start us, length us, event | category | flops | bytes accessed | tf_op | source)
XLA Modules:
  0.0 475.4 jit_solution(6904821887116888132)
XLA Ops:
  0.0 414.7 %reduce.1 = (bf16[4,1280,4096]{2,1,0:T(8,128)(2,1)}, bf16[2,256,512]{2,1,0:T(8,128)(2,1)}, bf16[2,256,512]{2,1,0:T(8,128)(2,1)}, bf16[2,256,512]{2,1,0:T(8,128)(...) custom-call(bf16[4,4096,1280]{2,1,0:T(8,128)(2,1)} %bitcast.2, ...), custom_call_target="tpu_custom_call" | custom-call | flops 171798691840 | bytes 218103808 | tf_op jit(solution)/shard_map/reduce/pallas_call | solution.py:511
  414.7 0.5 collective-permute-start.1
  415.1 1.3 collective-permute-start
  416.4 0.0 copy-start.4
  416.5 26.4 %move.1._ = bf16[4,1280,4096]{2,1,0:T(8,128)(2,1)} custom-call(bf16[4,1280,4096]{2,1,0:T(8,128)(2,1)} %get-tuple-element.21.res), custom_call_target="tpu_custom_call" | custom-call | flops 10000000000 | bytes 83886080 | tf_op jit(solution)/shard_map/move/pallas_call | solution.py:517
  442.9 0.0 collective-permute-done.lent
  443.0 0.9 settle_late.1._
  443.9 0.0 collective-permute-done.1.got
  443.9 3.6 collective-permute-start.2
  447.6 0.0 copy-done.2
  447.6 1.6 collective-permute-start.3
  449.2 0.7 collective-permute-done.2.lent
  449.9 0.0 copy-done.1
  449.9 1.5 shard_map.28._
  451.3 13.0 %collective-permute-done.3.got = bf16[5,128,512]{2,1,0:T(8,128)(2,1)S(1)} collective-permute-done((bf16[5,128,512]{2,1,0:T(8,128)(2,1)S(1)}, bf16[5,128,512]{2,1,0:T(8,128)(2,1)S(1)}, u32[]{:S(2)}, u32[]{:S(2)}) %collective-permute-start.3) | collective-permute-done | bytes 655392 | tf_op jit(solution)/shard_map/ppermute | solution.py:515
  464.3 0.0 collective-permute-start.4
  464.3 0.0 copy-done.7
  464.3 1.6 collective-permute-start.5
  465.9 0.5 collective-permute-done.4.lent
  466.4 1.2 shard_map.29._
  467.6 5.5 %collective-permute-done.5.got = bf16[2,128,512]{2,1,0:T(8,128)(2,1)S(1)} collective-permute-done((bf16[2,128,512]{2,1,0:T(8,128)(2,1)S(1)}, bf16[2,128,512]{2,1,0:T(8,128)(2,1)S(1)}, u32[]{:S(2)}, u32[]{:S(2)}) %collective-permute-start.5) | collective-permute-done | bytes 262176 | tf_op jit(solution)/shard_map/ppermute | solution.py:515
  473.0 0.0 collective-permute-start.6
  473.0 1.5 collective-permute-done.6.lent
  474.6 0.9 shard_map.30
  (14 shorter events, 0.0 us)
Async XLA Ops:
  414.7 29.2 %collective-permute-start.1 = (bf16[8,128,512]{2,1,0:T(8,128)(2,1)}, bf16[8,128,512]{2,1,0:T(8,128)(2,1)S(1)}, u32[]{:S(2)}, u32[]{:S(2)}) collective-permute-start(bf16[8,128,512]{2,1,0:T(8,128)(2,1)} %get-tuple-element.25.own), channel_id=1, source_target_pairs={{0,2},{1,3},{2,0},{3,1},{4,6},{5,7},{6,4},{7,5}} | collective-permute-start | bytes 3145736 | tf_op jit(solution)/shard_map/ppermute | solution.py:515
  415.1 27.8 %collective-permute-start = (bf16[2,256,512]{2,1,0:T(8,128)(2,1)}, bf16[2,256,512]{2,1,0:T(8,128)(2,1)S(1)}, u32[]{:S(2)}, u32[]{:S(2)}) collective-permute-start(bf16[2,256,512]{2,1,0:T(8,128)(2,1)} %get-tuple-element.24.got), channel_id=1, source_target_pairs={{1,0},{3,2},{5,4},{7,6}} | collective-permute-start | bytes 1572872 | tf_op jit(solution)/shard_map/ppermute | solution.py:516
  416.4 26.5 %copy-start.4 = (bf16[2,256,512]{2,1,0:T(8,128)(2,1)S(1)}, bf16[2,256,512]{2,1,0:T(8,128)(2,1)}, u32[]{:S(2)}) copy-start(bf16[2,256,512]{2,1,0:T(8,128)(2,1)} %get-tuple-element.22.own) | copy-start | bytes 1572868
  416.4 26.5 %copy-start.5 = (bf16[2,256,512]{2,1,0:T(8,128)(2,1)S(1)}, bf16[2,256,512]{2,1,0:T(8,128)(2,1)}, u32[]{:S(2)}) copy-start(bf16[2,256,512]{2,1,0:T(8,128)(2,1)} %get-tuple-element.23.sib) | copy-start | bytes 1572868
  416.4 26.5 %copy-start.6 = (bf16[2,256,512]{2,1,0:T(8,128)(2,1)S(1)}, bf16[2,256,512]{2,1,0:T(8,128)(2,1)}, u32[]{:S(2)}) copy-start(bf16[2,256,512]{2,1,0:T(8,128)(2,1)} %get-tuple-element.24.got) | copy-start | bytes 1572868
  442.9 4.6 copy-start.2
  443.0 6.9 %copy-start = (bf16[8,128,512]{2,1,0:T(8,128)(2,1)S(1)}, bf16[8,128,512]{2,1,0:T(8,128)(2,1)}, u32[]{:S(2)}) copy-start(bf16[8,128,512]{2,1,0:T(8,128)(2,1)} %get-tuple-element.25.own) | copy-start | bytes 3145732
  443.0 6.9 %copy-start.1 = (bf16[8,128,512]{2,1,0:T(8,128)(2,1)S(1)}, bf16[8,128,512]{2,1,0:T(8,128)(2,1)}, u32[]{:S(2)}) copy-start(bf16[8,128,512]{2,1,0:T(8,128)(2,1)} %get-tuple-element.27.sib) | copy-start | bytes 3145732
  443.9 5.9 %collective-permute-start.2 = (bf16[8,128,512]{2,1,0:T(8,128)(2,1)S(1)}, bf16[8,128,512]{2,1,0:T(8,128)(2,1)S(1)}, u32[]{:S(2)}, u32[]{:S(2)}) collective-permute-start(bf16[8,128,512]{2,1,0:T(8,128)(2,1)S(1)} %collective-permute-done.1.got), channel_id=1, source_target_pairs={{0,1},{1,0},{2,3},{3,2},{4,5},{5,4},{6,7},{7,6}} | collective-permute-start | bytes 3145736 | tf_op jit(solution)/shard_map/ppermute | solution.py:521
  447.6 16.7 %collective-permute-start.3 = (bf16[5,128,512]{2,1,0:T(8,128)(2,1)S(1)}, bf16[5,128,512]{2,1,0:T(8,128)(2,1)S(1)}, u32[]{:S(2)}, u32[]{:S(2)}) collective-permute-start(bf16[5,128,512]{2,1,0:T(8,128)(2,1)S(1)} %copy-done.2), channel_id=1, source_target_pairs={{0,2},{1,3},{2,0},{3,1},{4,6},{5,7},{6,4},{7,5}} | collective-permute-start | bytes 1966088 | tf_op jit(solution)/shard_map/ppermute | solution.py:515
  449.9 14.4 %copy-start.7 = (bf16[2,128,512]{2,1,0:T(8,128)(2,1)S(1)}, bf16[2,128,512]{2,1,0:T(8,128)(2,1)}, u32[]{:S(2)}) copy-start(bf16[2,128,512]{2,1,0:T(8,128)(2,1)} %get-tuple-element.33.own) | copy-start | bytes 786436
  449.9 16.5 %copy-start.3 = (bf16[5,128,512]{2,1,0:T(8,128)(2,1)S(1)}, bf16[5,128,512]{2,1,0:T(8,128)(2,1)}, u32[]{:S(2)}) copy-start(bf16[5,128,512]{2,1,0:T(8,128)(2,1)} %get-tuple-element.31.sib) | copy-start | bytes 1966084
  464.3 2.1 collective-permute-start.4
  464.3 8.7 %collective-permute-start.5 = (bf16[2,128,512]{2,1,0:T(8,128)(2,1)S(1)}, bf16[2,128,512]{2,1,0:T(8,128)(2,1)S(1)}, u32[]{:S(2)}, u32[]{:S(2)}) collective-permute-start(bf16[2,128,512]{2,1,0:T(8,128)(2,1)S(1)} %copy-done.7), channel_id=1, source_target_pairs={{0,2},{1,3},{2,0},{3,1},{4,6},{5,7},{6,4},{7,5}} | collective-permute-start | bytes 786440 | tf_op jit(solution)/shard_map/ppermute | solution.py:515
  466.4 8.2 %copy-start.8 = (bf16[2,128,512]{2,1,0:T(8,128)(2,1)S(1)}, bf16[2,128,512]{2,1,0:T(8,128)(2,1)}, u32[]{:S(2)}) copy-start(bf16[2,128,512]{2,1,0:T(8,128)(2,1)} %get-tuple-element.35.sib) | copy-start | bytes 786436
  473.0 1.5 collective-permute-start.6
